TPU v7x, 32 devices: a whole 2x2x4 slice. The times are simulated.
32 devices in a mesh: band: 8 (over z, y), ga: 4 (over x, core).
Axes of the slice: x: 2, y: 2, z: 4, core: 2. Of those that a mesh axis runs over, the one named last changes fastest.
Arguments:
- orbitals: float32 [8, 96, 9216], P('band', 'ga'), may hold values from -6 to 6
- retained: int32 [96, 9216], P(None, 'ga'), may hold values 0 or 1
Outputs:
- exchange_field: float32 [8, 96, 9216], P('band', 'ga')
- block_matrix: float32 [8, 1], P('band')
All inputs are finite; a program needn't handle non-finite values. No bound on the sum of `retained` on one device may be relied on, other than what follows from the above.
Results may differ from a plain program's by a relative error of at most 0.0086.
Values may be sent and summed in bfloat16 or wider, within the bound.
No kernel may reach another device: no remote copies, remote signals or barrier semaphores. Data moves between devices by JAX's collectives and lax.ppermute only.
A program may use at most 64 MiB of HBM per device.

v0:
```python
import jax
import jax.numpy as jnp
from jax import lax
from jax.sharding import PartitionSpec as P


def passed_along(value, axis, steps):
    count = lax.axis_size(axis)
    pairs = [(source, (source + steps) % count) for source in range(count)]
    return lax.ppermute(value, axis, pairs)


def cas_table(length):
    counter = jnp.arange(length, dtype=jnp.int32)
    product = counter[:, None] * counter[None, :] % length
    angles = 2.0 * jnp.pi / length * product.astype(jnp.float32)
    scaled = (jnp.cos(angles) + jnp.sin(angles)) / jnp.sqrt(jnp.float32(length))
    return scaled.astype(jnp.bfloat16)


def wrapped(indices, length):
    return jnp.where(indices < length // 2, indices, indices - length).astype(jnp.float32)


def screening(rows_x, rows_y, rows_z, length):
    freq_x = wrapped(rows_x, length)
    freq_y = wrapped(rows_y, length)
    freq_z = wrapped(rows_z, length)
    squared = freq_x[:, None, None] ** 2 + freq_y[None, :, None] ** 2 + freq_z[None, None, :] ** 2
    spread = length / 4.0
    return 1.0 / (1.0 + squared / (spread * spread))


def transform_axis(density, table, form):
    return jnp.einsum(form, density, table, preferred_element_type=jnp.float32).astype(jnp.bfloat16)


def local(orbitals, retained):
    bands_dev, slab_rows, plane_cells = orbitals.shape
    length = retained.shape[0]
    groups = lax.axis_size("ga")
    column_rows = length // groups
    lattice = orbitals.reshape(bands_dev, slab_rows, length, length)
    table = cas_table(length)
    counter = jnp.arange(length, dtype=jnp.int32)
    local_y = lax.axis_index("ga") * column_rows + jnp.arange(column_rows, dtype=jnp.int32)
    screen = screening(counter, local_y, counter, length) * retained.reshape(
        length, column_rows, length
    ).astype(jnp.float32)

    def potentials(density):
        sectioned = transform_axis(density, table, "pxyz,kz->pxyk")
        sectioned = transform_axis(sectioned, table, "pxyz,ky->pxkz")
        spectrum = transform_axis(
            lax.all_to_all(sectioned, "ga", split_axis=2, concat_axis=1, tiled=True),
            table,
            "pxyz,kx->pkyz",
        )
        spectrum = (spectrum.astype(jnp.float32) * screen).astype(jnp.bfloat16)
        spectrum = transform_axis(spectrum, table, "pxyz,kx->pkyz")
        returned = lax.all_to_all(spectrum, "ga", split_axis=1, concat_axis=2, tiled=True)
        returned = transform_axis(returned, table, "pxyz,ky->pxkz")
        return transform_axis(returned, table, "pxyz,kz->pxyk")

    def interact(visitors):
        visit_count = visitors.shape[0]
        density = (lattice[:, None] * visitors[None]).astype(jnp.bfloat16)
        density = density.reshape(bands_dev * visit_count, slab_rows, length, length)
        fields = potentials(density).astype(jnp.float32)
        return fields.reshape(bands_dev, visit_count, slab_rows, length, length)

    band_reach = max(1, lax.axis_size("band") // 8)
    running = jnp.sum(interact(lattice) * lattice[None], axis=1)
    visitors = passed_along(lattice.astype(jnp.bfloat16), "band", 1).astype(lattice.dtype)
    fields = interact(visitors)
    running = running + jnp.sum(fields * visitors[None], axis=1)
    carried = jnp.sum(fields * lattice[:, None], axis=0)

    def round_once(rounds_done, state_tuple):
        visiting, partial_field, running_sum = state_tuple
        visiting, partial_field = (
            passed_along(visiting.astype(jnp.bfloat16), "band", 1).astype(visiting.dtype),
            passed_along(partial_field.astype(jnp.bfloat16), "band", 1).astype(partial_field.dtype),
        )
        fields_now = interact(visiting)
        partial_field = partial_field + jnp.sum(fields_now * lattice[:, None], axis=0)
        running_sum = running_sum + jnp.sum(fields_now * visiting[None], axis=1)
        return (visiting, partial_field, running_sum)

    visitors, carried, running = lax.fori_loop(
        1, band_reach, round_once, (visitors, carried, running)
    )
    running = running + passed_along(carried.astype(jnp.bfloat16), "band", -band_reach).astype(
        carried.dtype
    )
    flat_orbitals = lattice.reshape(bands_dev, -1)
    flat_running = running.reshape(bands_dev, -1)
    intersection = jnp.dot(flat_orbitals, flat_running.T, precision=lax.Precision.HIGHEST)
    intersection = lax.psum(intersection, "ga") / float(length**3)
    return (running.reshape(bands_dev, slab_rows, plane_cells), intersection)


def solution(mesh):
    placed = (P("band", "ga", None), P(None, "ga"))
    return jax.shard_map(
        local,
        mesh=mesh,
        in_specs=placed,
        out_specs=(P("band", "ga", None), P("band", None)),
        check_vma=False,
    )
```

profile of v0, /device:TPU:0, one launch (start us, length us, event | category | flops | bytes accessed | tf_op | source)
XLA Modules:
  0.0 101.4 jit_solution(7748749832442671103)
XLA Ops:
  0.6 1.6 %broadcast_in_dim_reshape.10 = f32[1,24,96,96]{3,2,1,0:T(8,128)S(1)} reshape(f32[1,24,9216]{2,1,0:T(8,128)} %param.2) | data formatting | bytes 1769472 | tf_op jit(solution)/shard_map/broadcast_in_dim;reshape | solution.py:67
  2.3 0.0 copy-start
  2.3 0.9 convert_element_type.234
  3.2 3.0 %collective-permute-start = (bf16[1,24,96,96]{3,2,1,0:T(8,128)(2,1)}, bf16[1,24,96,96]{3,2,1,0:T(8,128)(2,1)}, u32[]{:S(2)}, u32[]{:S(2)}) collective-permute-start(bf16[1,24,96,96]{3,2,1,0:T(8,128)(2,1)} %convert_element_type.234), channel_id=1, source_target_pairs={{0,4},{4,8},{8,12},{12,16},{16,20},{20,24},{24,28},{28,0},{1,5},{5... | collective-permute-start | bytes 1327112 | tf_op jit(solution)/shard_map/ppermute | solution.py:10
  6.2 0.0 copy-done
  6.2 0.5 broadcast_in_dim_reshape.4
  6.6 16.2 %collective-permute-done = bf16[1,24,96,96]{3,2,1,0:T(8,128)(2,1)} collective-permute-done((bf16[1,24,96,96]{3,2,1,0:T(8,128)(2,1)}, bf16[1,24,96,96]{3,2,1,0:T(8,128)(2,1)}, u32[]{:S(2)}, u32[]{:S(2)}) %collective-permute-start) | collective-permute-done | bytes 442400 | tf_op jit(solution)/shard_map/ppermute | solution.py:10
  22.8 2.7 %fusion.12 = bf16[1,24,96,96]{3,2,1,0:T(8,128)(2,1)} fusion(f32[1,24,96,96]{3,2,1,0:T(8,128)S(1)} %broadcast_in_dim_reshape.10, bf16[1,24,96,96]{3,2,1,0:T(8,128)(2,1)} %collective-permute-done), kind=kOutput, calls=%fused_computation.28 | convolution fusion | flops 86261760 | bytes 1769472 | tf_op jit(solution)/shard_map/pxyz,ky->pxkz/dot_general | solution.py:35
  25.5 2.1 %copy.27 = bf16[1,24,96,96]{3,1,0,2:T(8,128)(2,1)} copy(bf16[1,24,96,96]{3,2,1,0:T(8,128)(2,1)} %fusion.12) | data formatting | bytes 884736 | tf_op jit(solution)/shard_map/convert_element_type | solution.py:35
  27.6 3.5 %all-to-all-start.2 = ((bf16[1,24,96,96]{3,1,0,2:T(8,128)(2,1)}), bf16[1,24,96,96]{3,1,0,2:T(8,128)(2,1)S(1)}, u32[]{:S(2)}, u32[]{:S(2)}) async-start(bf16[1,24,96,96]{3,1,0,2:T(8,128)(2,1)} %copy.27), calls=%async_computation.2 | async-start | bytes 1179648 | tf_op jit(solution)/shard_map/all_to_all | solution.py:55
  31.1 0.8 fusion.9
  31.9 1.0 %copy.20 = bf16[1,24,96,96]{3,1,0,2:T(8,128)(2,1)} copy(bf16[1,24,96,96]{3,2,1,0:T(8,128)(2,1)S(1)} %fusion.9) | data formatting | bytes 884736 | tf_op jit(solution)/shard_map/convert_element_type | solution.py:35
  33.0 7.6 %all-to-all-done.2 = bf16[1,24,96,96]{3,1,0,2:T(8,128)(2,1)S(1)} async-done(((bf16[1,24,96,96]{3,1,0,2:T(8,128)(2,1)}), bf16[1,24,96,96]{3,1,0,2:T(8,128)(2,1)S(1)}, u32[]{:S(2)}, u32[]{:S(2)}) %all-to-all-start.2) | async-done | bytes 442400 | tf_op jit(solution)/shard_map/all_to_all | solution.py:55
  40.6 0.0 copy-start.4
  40.6 4.1 %all-to-all-start = ((bf16[1,24,96,96]{3,1,0,2:T(8,128)(2,1)}), bf16[1,24,96,96]{3,1,0,2:T(8,128)(2,1)}, u32[]{:S(2)}, u32[]{:S(2)}) async-start(bf16[1,24,96,96]{3,1,0,2:T(8,128)(2,1)} %copy.20), calls=%async_computation | async-start | bytes 1179648 | tf_op jit(solution)/shard_map/all_to_all | solution.py:55
  44.7 0.0 copy-done.4
  44.8 0.1 broadcast_add_fusion
  44.8 1.2 %convert_element_type.224 = f32[96,2304]{1,0:T(8,128)S(1)} convert(s32[96,2304]{1,0:T(8,128)} %param.3) | non-fusion elementwise | flops 221184 | bytes 1769472 | tf_op jit(solution)/shard_map/convert_element_type | solution.py:49
  46.1 1.8 %convert_element_type.225 = f32[96,24,96]{2,1,0:T(8,128)} reshape(f32[96,2304]{1,0:T(8,128)S(1)} %convert_element_type.224) | data formatting | bytes 1769472 | tf_op jit(solution)/shard_map/convert_element_type | solution.py:49
  47.9 1.1 %copy.28 = bf16[1,24,96,96]{3,2,1,0:T(8,128)(2,1)S(1)} copy(bf16[1,24,96,96]{3,1,0,2:T(8,128)(2,1)} %copy-done.4) | data formatting | bytes 884736 | tf_op jit(solution)/shard_map/all_to_all | solution.py:55
  49.1 0.1 copy.29
  49.1 2.1 %fusion.13 = bf16[1,96,24,96]{3,1,2,0:T(8,128)(2,1)S(1)} fusion(bf16[96,24,96]{2,1,0:T(8,128)(2,1)S(1)} %bitcast.96, f32[96,24,96]{2,1,0:T(8,128)} %convert_element_type.225, f32[96]{0:T(128)S(1)} %fusion.86, f32[96,24]{0,1:T(8,128)S(1)} %broadcast_add_fusion), kind=kOutput, calls=%fused_computation.29 | convolution fusion | flops 87367680 | bytes 1779072 | tf_op jit(solution)/shard_map/pxyz,kx->pkyz/dot_general | solution.py:35
  51.3 1.0 %copy.31 = bf16[1,96,24,96]{3,2,0,1:T(8,128)(2,1)} copy(bf16[1,96,24,96]{3,1,2,0:T(8,128)(2,1)S(1)} %fusion.13) | data formatting | bytes 884736 | tf_op jit(solution)/shard_map/convert_element_type | solution.py:35
  52.3 2.0 %all-to-all-done = bf16[1,24,96,96]{3,1,0,2:T(8,128)(2,1)} async-done(((bf16[1,24,96,96]{3,1,0,2:T(8,128)(2,1)}), bf16[1,24,96,96]{3,1,0,2:T(8,128)(2,1)}, u32[]{:S(2)}, u32[]{:S(2)}) %all-to-all-start) | async-done | bytes 442400 | tf_op jit(solution)/shard_map/all_to_all | solution.py:55
  54.3 3.5 %all-to-all-start.3 = ((bf16[1,96,24,96]{3,2,0,1:T(8,128)(2,1)}), bf16[1,96,24,96]{3,2,0,1:T(8,128)(2,1)S(1)}, u32[]{:S(2)}, u32[]{:S(2)}) async-start(bf16[1,96,24,96]{3,2,0,1:T(8,128)(2,1)} %copy.31), calls=%async_computation.3 | async-start | bytes 1179648 | tf_op jit(solution)/shard_map/all_to_all | solution.py:61
  57.8 1.1 %copy.21 = bf16[1,24,96,96]{3,2,1,0:T(8,128)(2,1)S(1)} copy(bf16[1,24,96,96]{3,1,0,2:T(8,128)(2,1)} %all-to-all-done) | data formatting | bytes 884736 | tf_op jit(solution)/shard_map/all_to_all | solution.py:55
  59.0 0.9 copy.22
  59.9 7.4 %all-to-all-done.3 = bf16[1,96,24,96]{3,2,0,1:T(8,128)(2,1)S(1)} async-done(((bf16[1,96,24,96]{3,2,0,1:T(8,128)(2,1)}), bf16[1,96,24,96]{3,2,0,1:T(8,128)(2,1)S(1)}, u32[]{:S(2)}, u32[]{:S(2)}) %all-to-all-start.3) | async-done | bytes 442400 | tf_op jit(solution)/shard_map/all_to_all | solution.py:61
  67.3 0.1 copy.32
  67.4 0.7 convolution_convert_fusion
  68.1 0.0 copy-start.1
  68.1 1.0 fusion.19
  69.1 0.0 copy-done.1
  69.1 1.7 %collective-permute-start.1 = (bf16[1,24,96,96]{3,2,1,0:T(8,128)(2,1)}, bf16[1,24,96,96]{3,2,1,0:T(8,128)(2,1)S(1)}, u32[]{:S(2)}, u32[]{:S(2)}) collective-permute-start(bf16[1,24,96,96]{3,2,1,0:T(8,128)(2,1)} %fusion.19), channel_id=1, source_target_pairs={{0,28},{4,0},{8,4},{12,8},{16,12},{20,16},{24,20},{28,24},{1,29},{... | collective-permute-start | bytes 1327112 | tf_op jit(solution)/shard_map/ppermute | solution.py:10
  70.8 2.3 %fusion.10 = bf16[1,96,24,96]{3,1,2,0:T(8,128)(2,1)S(1)} fusion(bf16[96,24,96]{2,1,0:T(8,128)(2,1)} %bitcast.95, f32[96,24,96]{2,1,0:T(8,128)} %convert_element_type.225, f32[96]{0:T(128)S(1)} %fusion.86, f32[96,24]{0,1:T(8,128)S(1)} %broadcast_add_fusion), kind=kOutput, calls=%fused_computation.26 | convolution fusion | flops 87367680 | bytes 1779072 | tf_op jit(solution)/shard_map/pxyz,kx->pkyz/dot_general | solution.py:35
  73.2 1.1 %copy.25 = bf16[1,96,24,96]{3,2,0,1:T(8,128)(2,1)} copy(bf16[1,96,24,96]{3,1,2,0:T(8,128)(2,1)S(1)} %fusion.10) | data formatting | bytes 884736 | tf_op jit(solution)/shard_map/convert_element_type | solution.py:35
  74.2 3.5 %all-to-all-start.1 = ((bf16[1,96,24,96]{3,2,0,1:T(8,128)(2,1)}), bf16[1,96,24,96]{3,2,0,1:T(8,128)(2,1)S(1)}, u32[]{:S(2)}, u32[]{:S(2)}) async-start(bf16[1,96,24,96]{3,2,0,1:T(8,128)(2,1)} %copy.25), calls=%async_computation.1 | async-start | bytes 1179648 | tf_op jit(solution)/shard_map/all_to_all | solution.py:61
  77.7 1.1 %copy.35 = f32[3,72,8,128]{3,1,2,0:T(8,128)} copy(f32[3,72,8,128]{3,2,1,0:T(8,128)S(1)} %bitcast.87) | data formatting | bytes 1769472
  78.8 0.0 copy-start.2
  78.8 8.4 %all-to-all-done.1 = bf16[1,96,24,96]{3,2,0,1:T(8,128)(2,1)S(1)} async-done(((bf16[1,96,24,96]{3,2,0,1:T(8,128)(2,1)}), bf16[1,96,24,96]{3,2,0,1:T(8,128)(2,1)S(1)}, u32[]{:S(2)}, u32[]{:S(2)}) %all-to-all-start.1) | async-done | bytes 442400 | tf_op jit(solution)/shard_map/all_to_all | solution.py:61
  87.2 0.1 copy.26
  87.3 0.0 collective-permute-done.1
  87.3 0.0 copy-start.5
  87.3 0.8 copy-done.5
  88.1 0.0 copy-done.2
  88.1 2.0 %fusion.17 = f32[1,24,96,96]{3,2,1,0:T(8,128)S(1)} fusion(bf16[1,24,96,96]{3,2,1,0:T(8,128)(2,1)} %collective-permute-done, bf16[24,96,96]{2,1,0:T(8,128)(2,1)S(1)} %copy-done.2, bf16[1,24,96,96]{3,2,1,0:T(8,128)(2,1)} %copy-done.5, f32[24,96,96]{2,1,0:T(8,128)S(1)} %broadcast_in_dim_reshape.4, bf16[24,96,96]{2,1,0:T(8,128)(2,1)S(1)} %bitcast.89), kind=kOutput, calls=%fused_computation.33 | convolution fusion | flops 87367680 | bytes 3538944 | tf_op jit(solution)/shard_map/pxyz,kz->pxyk/dot_general | solution.py:35
  90.1 0.7 reshape.226
  90.8 0.0 copy-start.3
  90.8 1.6 %reshape.225 = f32[1,24,9216]{2,1,0:T(8,128)} reshape(f32[1,24,96,96]{3,2,1,0:T(8,128)S(1)} %fusion.17) | data formatting | bytes 1769472 | tf_op jit(solution)/shard_map/reshape | solution.py:100
  92.4 0.0 copy-done.3
  92.4 0.8 multiply_reduce_fusion
  93.3 6.4 %psum.7 = f32[1,1]{1,0:T(1,128)} all-reduce(f32[1,1]{1,0:T(1,128)} %bitcast.29), channel_id=1, replica_groups=mesh['band'=8,'ga'=4] {'ga'}, use_global_device_ids=true, to_apply=%region_0.1 | all-reduce | flops 1 | bytes 8 | tf_op jit(solution)/shard_map/psum | solution.py:99
  (2 shorter events, 0.0 us)
Async XLA Ops:
  2.3 3.9 %copy-start = (f32[1,24,9216]{2,1,0:T(8,128)S(1)}, f32[1,24,9216]{2,1,0:T(8,128)}, u32[]{:S(2)}) copy-start(f32[1,24,9216]{2,1,0:T(8,128)} %param.2) | copy-start | bytes 2654212
  3.2 19.7 %collective-permute-start = (bf16[1,24,96,96]{3,2,1,0:T(8,128)(2,1)}, bf16[1,24,96,96]{3,2,1,0:T(8,128)(2,1)}, u32[]{:S(2)}, u32[]{:S(2)}) collective-permute-start(bf16[1,24,96,96]{3,2,1,0:T(8,128)(2,1)} %convert_element_type.234), channel_id=1, source_target_pairs={{0,4},{4,8},{8,12},{12,16},{16,20},{20,24},{24,28},{28,0},{1,5},{5... | collective-permute-start | bytes 1327112 | tf_op jit(solution)/shard_map/ppermute | solution.py:10
  27.6 13.0 %all-to-all-start.2 = ((bf16[1,24,96,96]{3,1,0,2:T(8,128)(2,1)}), bf16[1,24,96,96]{3,1,0,2:T(8,128)(2,1)S(1)}, u32[]{:S(2)}, u32[]{:S(2)}) async-start(bf16[1,24,96,96]{3,1,0,2:T(8,128)(2,1)} %copy.27), calls=%async_computation.2 | async-start | bytes 1179648 | tf_op jit(solution)/shard_map/all_to_all | solution.py:55
  40.6 4.2 %copy-start.4 = (bf16[1,24,96,96]{3,1,0,2:T(8,128)(2,1)}, bf16[1,24,96,96]{3,1,0,2:T(8,128)(2,1)S(1)}, u32[]{:S(2)}) copy-start(bf16[1,24,96,96]{3,1,0,2:T(8,128)(2,1)S(1)} %all-to-all-done.2) | copy-start | bytes 1327108
  40.6 13.7 %all-to-all-start = ((bf16[1,24,96,96]{3,1,0,2:T(8,128)(2,1)}), bf16[1,24,96,96]{3,1,0,2:T(8,128)(2,1)}, u32[]{:S(2)}, u32[]{:S(2)}) async-start(bf16[1,24,96,96]{3,1,0,2:T(8,128)(2,1)} %copy.20), calls=%async_computation | async-start | bytes 1179648 | tf_op jit(solution)/shard_map/all_to_all | solution.py:55
  54.3 13.0 %all-to-all-start.3 = ((bf16[1,96,24,96]{3,2,0,1:T(8,128)(2,1)}), bf16[1,96,24,96]{3,2,0,1:T(8,128)(2,1)S(1)}, u32[]{:S(2)}, u32[]{:S(2)}) async-start(bf16[1,96,24,96]{3,2,0,1:T(8,128)(2,1)} %copy.31), calls=%async_computation.3 | async-start | bytes 1179648 | tf_op jit(solution)/shard_map/all_to_all | solution.py:61
  68.1 1.0 copy-start.1
  69.1 18.2 %collective-permute-start.1 = (bf16[1,24,96,96]{3,2,1,0:T(8,128)(2,1)}, bf16[1,24,96,96]{3,2,1,0:T(8,128)(2,1)S(1)}, u32[]{:S(2)}, u32[]{:S(2)}) collective-permute-start(bf16[1,24,96,96]{3,2,1,0:T(8,128)(2,1)} %fusion.19), channel_id=1, source_target_pairs={{0,28},{4,0},{8,4},{12,8},{16,12},{20,16},{24,20},{28,24},{1,29},{... | collective-permute-start | bytes 1327112 | tf_op jit(solution)/shard_map/ppermute | solution.py:10
  74.2 13.0 %all-to-all-start.1 = ((bf16[1,96,24,96]{3,2,0,1:T(8,128)(2,1)}), bf16[1,96,24,96]{3,2,0,1:T(8,128)(2,1)S(1)}, u32[]{:S(2)}, u32[]{:S(2)}) async-start(bf16[1,96,24,96]{3,2,0,1:T(8,128)(2,1)} %copy.25), calls=%async_computation.1 | async-start | bytes 1179648 | tf_op jit(solution)/shard_map/all_to_all | solution.py:61
  78.8 9.3 %copy-start.2 = (bf16[24,96,96]{2,1,0:T(8,128)(2,1)S(1)}, bf16[24,96,96]{2,1,0:T(8,128)(2,1)}, u32[]{:S(2)}) copy-start(bf16[24,96,96]{2,1,0:T(8,128)(2,1)} %copy-done.1) | copy-start | bytes 1327108
  87.3 0.8 copy-start.5
  90.8 1.6 %copy-start.3 = (f32[3,72,8,128]{3,1,2,0:T(8,128)S(1)}, f32[3,72,8,128]{3,1,2,0:T(8,128)}, u32[]{:S(2)}) copy-start(f32[3,72,8,128]{3,1,2,0:T(8,128)} %copy.35) | copy-start | bytes 2654212
where the time goes:
time: 102 us; the launch traced here: 101 us
  waiting for transfers between devices  41.7 us (41%)
  starting transfers between devices  19.3 us (19%)
  local copies, waits for them, and re-layouts  16.8 us (16%)
  matrix products  10.7 us (10%)
  blocking collectives  6.37 us (6%)
  other arithmetic  4.03 us (4%)
  between operations  2.59 us (3%)
    ppermute x2, waiting for transfers between devices, passed_along(): return lax.ppermute(value, axis, pairs)  16.2 us
    all_to_all x2, waiting for transfers between devices, potentials(): lax.all_to_all(spectrum, 'ga', split_axis=1, concat_axis=2, tiled=True)  15.8 us
    dot_general x6, matrix products, transform_axis(): jnp.einsum(form, density, table, preferred_element_type=jnp.float32)  10.7 us
    all_to_all x2, waiting for transfers between devices, potentials(): lax.all_to_all(sectioned, 'ga', split_axis=2, concat_axis=1, tiled=True)  9.63 us
    all_to_all x2, starting transfers between devices, potentials(): lax.all_to_all(sectioned, 'ga', split_axis=2, concat_axis=1, tiled=True)  7.62 us
    all_to_all x2, starting transfers between devices, potentials(): lax.all_to_all(spectrum, 'ga', split_axis=1, concat_axis=2, tiled=True)  6.95 us
    psum x1, blocking collectives, local(): intersection = lax.psum(intersection, 'ga') / float(length ** 3)  6.37 us
    convert_element_type x4, local copies, waits for them, and re-layouts, transform_axis(): jnp.einsum(form, density, table, preferred_element_type=jnp.float32)  5.27 us
  transfers between devices with their start and end apart: 6, of which 5 were waited for; matrix products, arithmetic and copies ran while one was open for 16% of the time, Pallas kernels for 0%

commit v1 on v0

v1 whole, which is shorter than its diff:
```python
import math
from functools import partial

import jax
import jax.numpy as jnp
import numpy as np
from jax import lax
from jax.experimental import pallas as pl
from jax.experimental.pallas import tpu as pltpu
from jax.sharding import PartitionSpec as P

LANES = 128


def passed_along(value, axis, steps):
    count = lax.axis_size(axis)
    pairs = [(source, (source + steps) % count) for source in range(count)]
    return lax.ppermute(value, axis, pairs)


def cas_table(length):
    counter = np.arange(length)
    angles = 2.0 * np.pi / length * (counter[:, None] * counter[None, :] % length)
    scaled = (np.cos(angles) + np.sin(angles)) / np.sqrt(float(length))
    return scaled.astype(np.float32).astype(jnp.bfloat16).astype(np.float32)


def wrapped(indices, length):
    return jnp.where(indices < length // 2, indices, indices - length).astype(jnp.float32)


def screening(rows_x, rows_y, rows_z, length):
    freq_x = wrapped(rows_x, length)
    freq_y = wrapped(rows_y, length)
    freq_z = wrapped(rows_z, length)
    squared = freq_x[:, None, None] ** 2 + freq_y[None, :, None] ** 2 + freq_z[None, None, :] ** 2
    spread = length / 4.0
    return 1.0 / (1.0 + squared / (spread * spread))


def lane_of(shape):
    return lax.broadcasted_iota(jnp.int32, shape, len(shape) - 1)


def dense(parts, length):
    spill = LANES - length
    lane = lane_of(parts[0].shape)
    last = parts[-1]
    return [
        jnp.where(lane < length, part, pltpu.roll(last, (length - spill * j) % LANES, last.ndim - 1))
        for j, part in enumerate(parts[:-1])
    ]


def undense(parts, length):
    spill = LANES - length
    lane = lane_of(parts[0].shape)
    last = jnp.zeros_like(parts[0])
    for j, part in enumerate(parts):
        moved = pltpu.roll(part, (spill * j - length) % LANES, part.ndim - 1)
        last = jnp.where((lane >= spill * j) & (lane < spill * (j + 1)), moved, last)
    return last


def dot(a, b):
    return jnp.dot(a, b, preferred_element_type=jnp.float32)


class Sizes:
    def __init__(self, length, rows, groups):
        self.length = length
        self.rows = rows
        self.groups = groups
        self.cols = length // groups
        whole = math.lcm(length, LANES)
        self.pack = whole // length
        self.chunks = whole // LANES
        self.quads = length // self.pack
        self.width = self.pack * length
        self.inner = rows // self.pack
        assert self.chunks == self.pack - 1 and self.inner % 2 == 0 and self.cols % 2 == 0
        self.sent = (groups, self.chunks, self.inner * self.cols, LANES)


def tables(sz):
    table = cas_table(sz.length)
    spread = np.zeros((sz.width, sz.pack * LANES), np.float32)
    for r in range(sz.pack):
        spread[r * sz.length:(r + 1) * sz.length, r * LANES:r * LANES + sz.length] = table
    y_order = np.arange(sz.length).reshape(sz.quads, sz.pack).T.reshape(-1)
    x_all = np.arange(sz.length).reshape(sz.groups, sz.pack, sz.inner)
    x_order = x_all.transpose(1, 0, 2).reshape(-1)
    half = jnp.bfloat16
    return dict(
        z=jnp.asarray(spread, half), zb=jnp.asarray(spread.T, half),
        y=jnp.asarray(table[:, y_order], half), yb=jnp.asarray(table[y_order, :], half),
        x=jnp.asarray(table[:, x_order], half), xb=jnp.asarray(table[x_order, :], half),
    )


def forward_kernel(sz, a_ref, b_ref, z_ref, y_ref, out_ref, s_ref):
    w = sz.width
    rows = jnp.concatenate(
        [
            a_ref[:, q * w:(q + 1) * w] * b_ref[:, q * w:(q + 1) * w].astype(jnp.float32)
            for q in range(sz.quads)
        ],
        axis=0,
    ).astype(jnp.bfloat16)
    spread = dot(rows, z_ref[...])
    for r in range(sz.pack):
        s_ref[r] = spread[:, r * LANES:(r + 1) * LANES]
    for xi in range(0, sz.inner, 2):
        planes = []
        for g in range(sz.pack):
            col = jnp.concatenate(
                [
                    jnp.concatenate(
                        [
                            s_ref[r, pl.ds(g * sz.inner + xi + h, sz.quads, stride=sz.rows), :]
                            for r in range(sz.pack)
                        ],
                        axis=0,
                    )
                    for h in range(2)
                ],
                axis=1,
            ).astype(jnp.bfloat16)
            planes.append(dot(y_ref[...], col))
        packed = [
            dense([plane[:, h * LANES:(h + 1) * LANES] for plane in planes], sz.length)
            for h in range(2)
        ]
        for j in range(sz.chunks):
            for p in range(sz.groups):
                cut = slice(p * sz.cols, (p + 1) * sz.cols)
                out_ref[p, j, xi * sz.cols:(xi + 2) * sz.cols, :] = jnp.concatenate(
                    [packed[0][j][cut], packed[1][j][cut]], axis=0
                ).astype(jnp.bfloat16)


def middle_kernel(sz, r_ref, x_ref, xb_ref, screen_ref, out_ref, sum_ref, f_ref, g_ref):
    span = sz.inner * sz.cols
    for s in range(sz.groups):
        parts = [r_ref[s, j].astype(jnp.float32) for j in range(sz.chunks)]
        for g, part in enumerate(parts + [undense(parts, sz.length)]):
            f_ref[g, s * span:(s + 1) * span, :] = part
    many = sz.groups * sz.inner
    total = jnp.zeros((sz.length, LANES), jnp.float32)
    for ky in range(0, sz.cols, 2):
        col = jnp.concatenate(
            [
                jnp.concatenate(
                    [f_ref[g, pl.ds(ky + h, many, stride=sz.cols), :] for g in range(sz.pack)],
                    axis=0,
                )
                for h in range(2)
            ],
            axis=1,
        ).astype(jnp.bfloat16)
        spectrum = dot(x_ref[...], col).astype(jnp.bfloat16).astype(jnp.float32)
        screen = jnp.concatenate([screen_ref[ky], screen_ref[ky + 1]], axis=1)
        weighted = spectrum * screen
        energy = spectrum * weighted
        total = total + energy[:, :LANES] + energy[:, LANES:]
        back = dot(xb_ref[...], weighted.astype(jnp.bfloat16))
        for h in range(2):
            for g in range(sz.pack):
                g_ref[g, pl.ds(ky + h, many, stride=sz.cols), :] = back[
                    g * many:(g + 1) * many, h * LANES:(h + 1) * LANES
                ]
    sum_ref[...] = jnp.sum(total, axis=0, keepdims=True)
    for s in range(sz.groups):
        parts = [g_ref[g, s * span:(s + 1) * span, :] for g in range(sz.pack)]
        for j, part in enumerate(dense(parts, sz.length)):
            out_ref[s, j] = part.astype(jnp.bfloat16)


def backward_body(sz, r_ref, yb_ref, zb_ref, s_ref):
    for xi in range(0, sz.inner, 2):
        cut = slice(xi * sz.cols, (xi + 2) * sz.cols)
        blocks = []
        for p in range(sz.groups):
            parts = [r_ref[p, j, cut, :].astype(jnp.float32) for j in range(sz.chunks)]
            blocks.append(parts + [undense(parts, sz.length)])
        for g in range(sz.pack):
            col = jnp.concatenate(
                [
                    jnp.concatenate(
                        [blocks[p][g][h * sz.cols:(h + 1) * sz.cols] for p in range(sz.groups)],
                        axis=0,
                    )
                    for h in range(2)
                ],
                axis=1,
            ).astype(jnp.bfloat16)
            plane = dot(yb_ref[...], col)
            for h in range(2):
                for r in range(sz.pack):
                    s_ref[r, pl.ds(g * sz.inner + xi + h, sz.quads, stride=sz.rows), :] = plane[
                        r * sz.quads:(r + 1) * sz.quads, h * LANES:(h + 1) * LANES
                    ]
    rows = jnp.concatenate(
        [s_ref[r].astype(jnp.bfloat16) for r in range(sz.pack)], axis=1
    )
    return dot(rows, zb_ref[...]).astype(jnp.bfloat16).astype(jnp.float32)


def own_kernel(sz, r_ref, a_ref, yb_ref, zb_ref, out_ref, s_ref):
    v = backward_body(sz, r_ref, yb_ref, zb_ref, s_ref)
    for q in range(sz.quads):
        cut = slice(q * sz.width, (q + 1) * sz.width)
        out_ref[:, cut] = v[q * sz.rows:(q + 1) * sz.rows] * a_ref[:, cut]


def cross_kernel(sz, r_ref, a_ref, b_ref, run_ref, yb_ref, zb_ref, out_ref, back_ref, s_ref):
    v = backward_body(sz, r_ref, yb_ref, zb_ref, s_ref)
    for q in range(sz.quads):
        cut = slice(q * sz.width, (q + 1) * sz.width)
        part = v[q * sz.rows:(q + 1) * sz.rows]
        out_ref[:, cut] = run_ref[:, cut] + part * b_ref[:, cut].astype(jnp.float32)
        back_ref[:, cut] = (part * a_ref[:, cut]).astype(back_ref.dtype)


def local(orbitals, retained):
    bands_dev, slab_rows, plane_cells = orbitals.shape
    assert bands_dev == 1
    length = retained.shape[0]
    groups = lax.axis_size("ga")
    sz = Sizes(length, slab_rows, groups)
    tb = tables(sz)
    lattice = orbitals.reshape(slab_rows, plane_cells)
    half = jnp.bfloat16
    counter = jnp.arange(length, dtype=jnp.int32)
    local_y = lax.axis_index("ga") * sz.cols + jnp.arange(sz.cols, dtype=jnp.int32)
    screen = screening(counter, local_y, counter, length) * retained.reshape(
        length, sz.cols, length
    ).astype(jnp.float32)
    screen = jnp.pad(screen.transpose(1, 0, 2), ((0, 0), (0, 0), (0, LANES - length)))

    flat = (slab_rows, plane_cells)
    lines = pltpu.VMEM((sz.pack, sz.quads * sz.rows, LANES), jnp.float32)
    mids = pltpu.VMEM((sz.pack, sz.groups * sz.inner * sz.cols, LANES), jnp.float32)
    sent = jax.ShapeDtypeStruct(sz.sent, half)

    def to_spectrum(visitors):
        send = pl.pallas_call(
            partial(forward_kernel, sz), out_shape=sent, scratch_shapes=[lines], name="forward"
        )(lattice, visitors, tb["z"], tb["y"])
        got = lax.all_to_all(send, "ga", split_axis=0, concat_axis=0, tiled=True)
        send, total = pl.pallas_call(
            partial(middle_kernel, sz),
            out_shape=(sent, jax.ShapeDtypeStruct((1, LANES), jnp.float32)),
            scratch_shapes=[mids, mids],
            name="middle",
        )(got, tb["x"], tb["xb"], screen)
        return lax.all_to_all(send, "ga", split_axis=0, concat_axis=0, tiled=True), jnp.sum(total)

    def crossed(got, visitors, running):
        return pl.pallas_call(
            partial(cross_kernel, sz),
            out_shape=(
                jax.ShapeDtypeStruct(flat, jnp.float32),
                jax.ShapeDtypeStruct(flat, half),
            ),
            scratch_shapes=[lines],
            name="crossed",
        )(got, lattice, visitors, running, tb["yb"], tb["zb"])

    band_reach = max(1, lax.axis_size("band") // 8)
    visitors = passed_along(lattice.astype(half), "band", 1)
    got, own_total = to_spectrum(lattice)
    running = pl.pallas_call(
        partial(own_kernel, sz),
        out_shape=jax.ShapeDtypeStruct(flat, jnp.float32),
        scratch_shapes=[lines],
        name="own",
    )(got, lattice, tb["yb"], tb["zb"])
    got, total = to_spectrum(visitors)
    running, carried = crossed(got, visitors, running)
    own_total = own_total + total

    def round_once(rounds_done, state):
        visitors, carried, carried_total, running, own_total = state
        visitors = passed_along(visitors, "band", 1)
        carried = passed_along(carried, "band", 1)
        carried_total = passed_along(carried_total, "band", 1)
        got, total = to_spectrum(visitors)
        running, added = crossed(got, visitors, running)
        carried = (carried.astype(jnp.float32) + added.astype(jnp.float32)).astype(half)
        return visitors, carried, carried_total + total, running, own_total + total

    state = (visitors, carried, total, running, own_total)
    if band_reach > 1:
        state = lax.fori_loop(1, band_reach, round_once, state)
    visitors, carried, total, running, own_total = state
    returned = passed_along(carried, "band", -band_reach)
    intersection = own_total + passed_along(total, "band", -band_reach)
    intersection = lax.psum(intersection, "ga") / float(length**3)
    running = running + returned.astype(jnp.float32)
    return (running.reshape(orbitals.shape), intersection.reshape(1, 1))


def solution(mesh):
    placed = (P("band", "ga", None), P(None, "ga"))
    return jax.shard_map(
        local,
        mesh=mesh,
        in_specs=placed,
        out_specs=(P("band", "ga", None), P("band", None)),
        check_vma=False,
    )
```

time: 102 us -> 83.9 us (0.82)
  Pallas kernels: 0 us -> 19.3 us
  waiting for transfers between devices: 41.7 us -> 24.7 us
  local copies, waits for them, and re-layouts: 16.8 us -> 3.51 us
  matrix products: 10.7 us -> 0 us
  between operations: 2.59 us -> 4.41 us
  other arithmetic: 4.03 us -> 5.11 us
    pallas_call x0 -> x6, Pallas kernels: none -> 19.3 us  [the longest x2 6.29 us: to_spectrum(): pl.pallas_call(partial(forward_kernel, sz), out_shape=sent, scratch_shape...]
    all_to_all x4, waiting for transfers between devices: 25.4 us -> 11.9 us  [the longest x2 9.57 us: to_spectrum(): lax.all_to_all(send, 'ga', split_axis=0, concat_axis=0, tiled=True)]
    dot_general x6 -> x0, matrix products: 10.7 us -> none  [transform_axis(): jnp.einsum(form, density, table, preferred_element_type=jnp.float32)]
    convert_element_type x4 -> x0, local copies, waits for them, and re-layouts: 5.27 us -> none  [transform_axis(): jnp.einsum(form, density, table, preferred_element_type=jnp.float32)]
    ppermute x2 -> x3, waiting for transfers between devices: 16.2 us -> 12.8 us  [passed_along(): return lax.ppermute(value, axis, pairs)]
    all_to_all x6 -> x0, local copies, waits for them, and re-layouts: 3.38 us -> none  [the longest x4 3.26 us: potentials(): lax.all_to_all(sectioned, 'ga', split_axis=2, concat_axis=1, tiled=True)]
    another operation x3 -> x0, local copies, waits for them, and re-layouts: 2.79 us -> none  [the longest x2 2.09 us: interact(): density = (lattice[:, None] * visitors[None]).astype(jnp.bfloat16)]
    reshape x0 -> x1, other arithmetic: none -> 2.15 us  [local(): return (running.reshape(orbitals.shape), intersection.reshape(1, 1))]
  transfers between devices with their start and end apart: 6 -> 7, of which waited for: 5 -> 5; matrix products, arithmetic and copies ran while one was open for 16% -> 4% of each run, Pallas kernels for 0% -> 19%
where the time goes in v1:
time: 83.9 us; the launch traced here: 83.2 us
  waiting for transfers between devices  24.7 us (29%)
  starting transfers between devices  20 us (24%)
  Pallas kernels  19.3 us (23%)
  blocking collectives  6.17 us (7%)
  other arithmetic  5.11 us (6%)
  between operations  4.41 us (5%)
  local copies, waits for them, and re-layouts  3.51 us (4%)
    ppermute x3, waiting for transfers between devices, passed_along(): return lax.ppermute(value, axis, pairs)  12.8 us
    all_to_all x2, waiting for transfers between devices, to_spectrum(): lax.all_to_all(send, 'ga', split_axis=0, concat_axis=0, tiled=True)  9.57 us
    all_to_all x2, starting transfers between devices, to_spectrum(): got = lax.all_to_all(send, 'ga', split_axis=0, concat_axis=0, tiled=True)  6.93 us
    all_to_all x2, starting transfers between devices, to_spectrum(): lax.all_to_all(send, 'ga', split_axis=0, concat_axis=0, tiled=True)  6.93 us
    pallas_call x2, Pallas kernels, to_spectrum(): pl.pallas_call(partial(forward_kernel, sz), out_shape=sent, scratch_shape...  6.29 us
    ppermute x3, starting transfers between devices, passed_along(): return lax.ppermute(value, axis, pairs)  6.19 us
    psum x1, blocking collectives, local(): intersection = lax.psum(intersection, 'ga') / float(length ** 3)  6.17 us
    pallas_call x2, Pallas kernels, to_spectrum(): pl.pallas_call(partial(middle_kernel, sz), out_shape=(sent, jax.ShapeDtyp...  6.15 us
  transfers between devices with their start and end apart: 7, of which 5 were waited for; matrix products, arithmetic and copies ran while one was open for 4% of the time, Pallas kernels for 19%

profile of v1, /device:TPU:0, one launch (start us, length us, event | category | flops | bytes accessed | tf_op | source)
XLA Modules:
  0.0 83.2 jit_solution(16126015233023182847)
XLA Ops:
  0.6 1.2 %bitcast_convert_fusion = bf16[24,9216]{1,0:T(8,128)(2,1)S(1)} fusion(f32[1,24,9216]{2,1,0:T(8,128)} %param.8), kind=kLoop, calls=%fused_computation.10 | loop fusion | flops 221184 | bytes 1327104 | tf_op jit(solution)/shard_map/convert_element_type | solution.py:271
  1.8 3.0 %collective-permute-start = (bf16[24,9216]{1,0:T(8,128)(2,1)S(1)}, bf16[24,9216]{1,0:T(8,128)(2,1)S(1)}, u32[]{:S(2)}, u32[]{:S(2)}) collective-permute-start(bf16[24,9216]{1,0:T(8,128)(2,1)S(1)} %bitcast_convert_fusion), channel_id=1, source_target_pairs={{0,4},{4,8},{8,12},{12,16},{16,20},{20,24},{24,28},{28,0},{1,5},{5... | collective-permute-start | bytes 1327112 | tf_op jit(solution)/shard_map/ppermute | solution.py:18
  4.9 3.2 %forward.3 = bf16[4,3,144,128]{3,2,1,0:T(8,128)(2,1)} custom-call(f32[24,9216]{1,0:T(8,128)} %bitcast.7, f32[24,9216]{1,0:T(8,128)} %bitcast.8, bf16[384,512]{1,0:T(8,128)(2,1)} %constant.38.clone.z_ref, bf16[96,96]{1,0:T(8,128)(2,1)} %constant.40.clone.y_ref), custom_call_target="tpu_custom_call" | custom-call | tf_op jit(solution)/shard_map/forward/pallas_call | solution.py:247
  8.1 3.5 %all-to-all-start.2 = ((bf16[4,3,144,128]{3,2,1,0:T(8,128)(2,1)}), bf16[4,3,144,128]{3,2,1,0:T(8,128)(2,1)S(1)}, u32[]{:S(2)}, u32[]{:S(2)}) async-start(bf16[4,3,144,128]{3,2,1,0:T(8,128)(2,1)} %forward.3), calls=%async_computation.2 | async-start | bytes 884736 | tf_op jit(solution)/shard_map/all_to_all | solution.py:250
  11.6 0.0 copy-start.5
  11.6 6.5 %collective-permute-done.b_ref = bf16[24,9216]{1,0:T(8,128)(2,1)S(1)} collective-permute-done((bf16[24,9216]{1,0:T(8,128)(2,1)S(1)}, bf16[24,9216]{1,0:T(8,128)(2,1)S(1)}, u32[]{:S(2)}, u32[]{:S(2)}) %collective-permute-start) | collective-permute-done | bytes 442400 | tf_op jit(solution)/shard_map/ppermute | solution.py:18
  18.1 0.0 copy-start.3
  18.1 0.8 copy-done.3
  18.9 3.1 %forward.2 = bf16[4,3,144,128]{3,2,1,0:T(8,128)(2,1)} custom-call(f32[24,9216]{1,0:T(8,128)} %bitcast.9, bf16[24,9216]{1,0:T(8,128)(2,1)} %copy-done.3, bf16[384,512]{1,0:T(8,128)(2,1)} %constant.38.clone.z_ref, bf16[96,96]{1,0:T(8,128)(2,1)} %constant.40.clone.y_ref), custom_call_target="tpu_custom_call" | custom-call | tf_op jit(solution)/shard_map/forward/pallas_call | solution.py:247
  22.0 0.0 all-to-all-done.2.r_ref
  22.0 0.0 copy-start
  22.0 3.5 %all-to-all-start = ((bf16[4,3,144,128]{3,2,1,0:T(8,128)(2,1)}), bf16[4,3,144,128]{3,2,1,0:T(8,128)(2,1)S(1)}, u32[]{:S(2)}, u32[]{:S(2)}) async-start(bf16[4,3,144,128]{3,2,1,0:T(8,128)(2,1)} %forward.2), calls=%async_computation | async-start | bytes 884736 | tf_op jit(solution)/shard_map/all_to_all | solution.py:250
  25.4 0.1 broadcast_add_fusion
  25.5 0.0 copy-done.5
  25.5 0.1 convert_element_type.38
  25.6 0.0 copy-done
  25.6 0.8 convert_element_type.39
  26.4 0.4 fusion
  26.8 1.1 %pad.4.screen_ref = f32[24,96,128]{2,1,0:T(8,128)} pad(f32[24,96,96]{2,1,0:T(8,128)S(1)} %fusion, f32[]{:T(128)} %constant.36.clone.1), padding=0_0x0_0x0_32 | pad | bytes 2064388 | tf_op jit(solution)/shard_map/jit(_pad)/pad | solution.py:239
  27.9 3.1 %middle.3 = (bf16[4,3,144,128]{3,2,1,0:T(8,128)(2,1)}, f32[1,128]{1,0:T(1,128)}) custom-call(bf16[4,3,144,128]{3,2,1,0:T(8,128)(2,1)} %copy-done, bf16[96,96]{1,0:T(8,128)(2,1)} %constant.42.clone.x_ref, bf16[96,96]{1,0:T(8,128)(2,1)} %constant.43.clone.xb_ref, f32[24,96,128]{2,1,0:T(8,128)} %pad.4.screen_ref), custom_call_target="tpu_custom_call" | custom-call | tf_op jit(solution)/shard_map/middle/pallas_call | solution.py:251
  31.0 2.3 %all-to-all-done.r_ref = bf16[4,3,144,128]{3,2,1,0:T(8,128)(2,1)S(1)} async-done(((bf16[4,3,144,128]{3,2,1,0:T(8,128)(2,1)}), bf16[4,3,144,128]{3,2,1,0:T(8,128)(2,1)S(1)}, u32[]{:S(2)}, u32[]{:S(2)}) %all-to-all-start) | async-done | bytes 442400 | tf_op jit(solution)/shard_map/all_to_all | solution.py:250
  33.3 0.0 copy-start.1
  33.3 3.5 %all-to-all-start.3 = ((bf16[4,3,144,128]{3,2,1,0:T(8,128)(2,1)}), bf16[4,3,144,128]{3,2,1,0:T(8,128)(2,1)S(1)}, u32[]{:S(2)}, u32[]{:S(2)}) async-start(bf16[4,3,144,128]{3,2,1,0:T(8,128)(2,1)} %get-tuple-element.9), calls=%async_computation.3 | async-start | bytes 884736 | tf_op jit(solution)/shard_map/all_to_all | solution.py:257
  36.8 0.0 copy-done.1
  36.8 3.1 %middle.2 = (bf16[4,3,144,128]{3,2,1,0:T(8,128)(2,1)}, f32[1,128]{1,0:T(1,128)}) custom-call(bf16[4,3,144,128]{3,2,1,0:T(8,128)(2,1)} %copy-done.1, bf16[96,96]{1,0:T(8,128)(2,1)} %constant.42.clone.x_ref, bf16[96,96]{1,0:T(8,128)(2,1)} %constant.43.clone.xb_ref, f32[24,96,128]{2,1,0:T(8,128)} %pad.4.screen_ref), custom_call_target="tpu_custom_call" | custom-call | tf_op jit(solution)/shard_map/middle/pallas_call | solution.py:251
  39.9 4.8 %all-to-all-done.3.r_ref = bf16[4,3,144,128]{3,2,1,0:T(8,128)(2,1)S(1)} async-done(((bf16[4,3,144,128]{3,2,1,0:T(8,128)(2,1)}), bf16[4,3,144,128]{3,2,1,0:T(8,128)(2,1)S(1)}, u32[]{:S(2)}, u32[]{:S(2)}) %all-to-all-start.3) | async-done | bytes 442400 | tf_op jit(solution)/shard_map/all_to_all | solution.py:257
  44.7 0.0 copy-start.2
  44.7 3.5 %all-to-all-start.1 = ((bf16[4,3,144,128]{3,2,1,0:T(8,128)(2,1)}), bf16[4,3,144,128]{3,2,1,0:T(8,128)(2,1)S(1)}, u32[]{:S(2)}, u32[]{:S(2)}) async-start(bf16[4,3,144,128]{3,2,1,0:T(8,128)(2,1)} %get-tuple-element.8), calls=%async_computation.1 | async-start | bytes 884736 | tf_op jit(solution)/shard_map/all_to_all | solution.py:257
  48.2 0.0 copy-done.2
  48.2 3.1 %own.1.run_ref = f32[24,9216]{1,0:T(8,128)} custom-call(bf16[4,3,144,128]{3,2,1,0:T(8,128)(2,1)} %copy-done.2, f32[24,9216]{1,0:T(8,128)} %bitcast.10, bf16[96,96]{1,0:T(8,128)(2,1)} %constant.41.clone.yb_ref, bf16[512,384]{1,0:T(8,128)(2,1)} %constant.39.clone.zb_ref), custom_call_target="tpu_custom_call" | custom-call | tf_op jit(solution)/shard_map/own/pallas_call | solution.py:273
  51.3 0.0 copy-start.6
  51.3 0.0 copy-start.7
  51.3 4.8 %all-to-all-done.1.r_ref = bf16[4,3,144,128]{3,2,1,0:T(8,128)(2,1)S(1)} async-done(((bf16[4,3,144,128]{3,2,1,0:T(8,128)(2,1)}), bf16[4,3,144,128]{3,2,1,0:T(8,128)(2,1)S(1)}, u32[]{:S(2)}, u32[]{:S(2)}) %all-to-all-start.1) | async-done | bytes 442400 | tf_op jit(solution)/shard_map/all_to_all | solution.py:257
  56.1 0.0 copy-start.4
  56.1 0.8 copy-done.4
  56.9 3.7 %crossed.1 = (f32[24,9216]{1,0:T(8,128)}, bf16[24,9216]{1,0:T(8,128)(2,1)}) custom-call(bf16[4,3,144,128]{3,2,1,0:T(8,128)(2,1)} %copy-done.4, f32[24,9216]{1,0:T(8,128)} %bitcast.11, bf16[24,9216]{1,0:T(8,128)(2,1)} %copy-done.3, f32[24,9216]{1,0:T(8,128)} %own.1.run_ref, bf16[96,96]{1,0:T(8,128)(2,1)} %constant.41.clone.yb_ref, ...), custom_call_target="tpu_custom_call" | custom-call | tf_op jit(solution)/shard_map/crossed/pallas_call | solution.py:260
  60.6 1.7 %collective-permute-start.1 = (bf16[24,9216]{1,0:T(8,128)(2,1)}, bf16[24,9216]{1,0:T(8,128)(2,1)S(1)}, u32[]{:S(2)}, u32[]{:S(2)}) collective-permute-start(bf16[24,9216]{1,0:T(8,128)(2,1)} %get-tuple-element.11), channel_id=1, source_target_pairs={{0,28},{4,0},{8,4},{12,8},{16,12},{20,16},{24,20},{28,24},{1,29},{... | collective-permute-start | bytes 1327112 | tf_op jit(solution)/shard_map/ppermute | solution.py:18
  62.3 0.0 copy-done.6
  62.3 0.6 reduce_sum.18
  62.9 0.0 copy-done.7
  62.9 0.6 reduce_sum.19
  63.5 1.4 %collective-permute-start.2 = (f32[]{:T(128)}, f32[]{:T(128)}, u32[]{:S(2)}, u32[]{:S(2)}) collective-permute-start(f32[]{:T(128)} %reduce_sum.19), channel_id=1, source_target_pairs={{0,28},{4,0},{8,4},{12,8},{16,12},{20,16},{24,20},{28,24},{1,29},{... | collective-permute-start | bytes 20 | tf_op jit(solution)/shard_map/ppermute | solution.py:18
  66.2 6.3 %collective-permute-done.2 = f32[]{:T(128)} collective-permute-done((f32[]{:T(128)}, f32[]{:T(128)}, u32[]{:S(2)}, u32[]{:S(2)}) %collective-permute-start.2) | collective-permute-done | bytes 36 | tf_op jit(solution)/shard_map/ppermute | solution.py:18
  73.1 6.2 %psum.7 = f32[]{:T(128)} all-reduce(f32[]{:T(128)S(6)} %add.82), channel_id=1, replica_groups=mesh['band'=8,'ga'=4] {'ga'}, use_global_device_ids=true, to_apply=%region_2.3 | all-reduce | flops 1 | bytes 8 | tf_op jit(solution)/shard_map/psum | solution.py:299
  79.9 0.0 collective-permute-done.1
  79.9 2.2 %add_bitcast_fusion = f32[1,24,9216]{2,1,0:T(8,128)} fusion(f32[24,9216]{1,0:T(8,128)} %get-tuple-element.10, bf16[24,9216]{1,0:T(8,128)(2,1)S(1)} %collective-permute-done.1), kind=kLoop, calls=%fused_computation.2 | loop fusion | flops 442368 | bytes 2211840 | tf_op jit(solution)/shard_map/reshape | solution.py:301
  (2 shorter events, 0.0 us)
Async XLA Ops:
  1.8 16.3 %collective-permute-start = (bf16[24,9216]{1,0:T(8,128)(2,1)S(1)}, bf16[24,9216]{1,0:T(8,128)(2,1)S(1)}, u32[]{:S(2)}, u32[]{:S(2)}) collective-permute-start(bf16[24,9216]{1,0:T(8,128)(2,1)S(1)} %bitcast_convert_fusion), channel_id=1, source_target_pairs={{0,4},{4,8},{8,12},{12,16},{16,20},{20,24},{24,28},{28,0},{1,5},{5... | collective-permute-start | bytes 1327112 | tf_op jit(solution)/shard_map/ppermute | solution.py:18
  8.1 13.8 %all-to-all-start.2 = ((bf16[4,3,144,128]{3,2,1,0:T(8,128)(2,1)}), bf16[4,3,144,128]{3,2,1,0:T(8,128)(2,1)S(1)}, u32[]{:S(2)}, u32[]{:S(2)}) async-start(bf16[4,3,144,128]{3,2,1,0:T(8,128)(2,1)} %forward.3), calls=%async_computation.2 | async-start | bytes 884736 | tf_op jit(solution)/shard_map/all_to_all | solution.py:250
  11.6 13.9 %copy-start.5 = (s32[96,2304]{1,0:T(8,128)S(1)}, s32[96,2304]{1,0:T(8,128)}, u32[]{:S(2)}) copy-start(s32[96,2304]{1,0:T(8,128)} %param.9) | copy-start | bytes 2654212
  18.1 0.8 copy-start.3
  22.0 3.6 %copy-start = (bf16[4,3,144,128]{3,2,1,0:T(8,128)(2,1)}, bf16[4,3,144,128]{3,2,1,0:T(8,128)(2,1)S(1)}, u32[]{:S(2)}) copy-start(bf16[4,3,144,128]{3,2,1,0:T(8,128)(2,1)S(1)} %all-to-all-done.2.r_ref) | copy-start | bytes 1327108
  22.0 11.4 %all-to-all-start = ((bf16[4,3,144,128]{3,2,1,0:T(8,128)(2,1)}), bf16[4,3,144,128]{3,2,1,0:T(8,128)(2,1)S(1)}, u32[]{:S(2)}, u32[]{:S(2)}) async-start(bf16[4,3,144,128]{3,2,1,0:T(8,128)(2,1)} %forward.2), calls=%async_computation | async-start | bytes 884736 | tf_op jit(solution)/shard_map/all_to_all | solution.py:250
  33.3 3.5 %copy-start.1 = (bf16[4,3,144,128]{3,2,1,0:T(8,128)(2,1)}, bf16[4,3,144,128]{3,2,1,0:T(8,128)(2,1)S(1)}, u32[]{:S(2)}) copy-start(bf16[4,3,144,128]{3,2,1,0:T(8,128)(2,1)S(1)} %all-to-all-done.r_ref) | copy-start | bytes 1327108
  33.3 11.4 %all-to-all-start.3 = ((bf16[4,3,144,128]{3,2,1,0:T(8,128)(2,1)}), bf16[4,3,144,128]{3,2,1,0:T(8,128)(2,1)S(1)}, u32[]{:S(2)}, u32[]{:S(2)}) async-start(bf16[4,3,144,128]{3,2,1,0:T(8,128)(2,1)} %get-tuple-element.9), calls=%async_computation.3 | async-start | bytes 884736 | tf_op jit(solution)/shard_map/all_to_all | solution.py:257
  44.7 3.5 %copy-start.2 = (bf16[4,3,144,128]{3,2,1,0:T(8,128)(2,1)}, bf16[4,3,144,128]{3,2,1,0:T(8,128)(2,1)S(1)}, u32[]{:S(2)}) copy-start(bf16[4,3,144,128]{3,2,1,0:T(8,128)(2,1)S(1)} %all-to-all-done.3.r_ref) | copy-start | bytes 1327108
  44.7 11.4 %all-to-all-start.1 = ((bf16[4,3,144,128]{3,2,1,0:T(8,128)(2,1)}), bf16[4,3,144,128]{3,2,1,0:T(8,128)(2,1)S(1)}, u32[]{:S(2)}, u32[]{:S(2)}) async-start(bf16[4,3,144,128]{3,2,1,0:T(8,128)(2,1)} %get-tuple-element.8), calls=%async_computation.1 | async-start | bytes 884736 | tf_op jit(solution)/shard_map/all_to_all | solution.py:257
  51.3 11.0 %copy-start.6 = (f32[1,128]{1,0:T(1,128)S(1)}, f32[1,128]{1,0:T(1,128)}, u32[]{:S(2)}) copy-start(f32[1,128]{1,0:T(1,128)} %get-tuple-element.12) | copy-start | bytes 1540
  51.3 11.6 %copy-start.7 = (f32[1,128]{1,0:T(1,128)S(1)}, f32[1,128]{1,0:T(1,128)}, u32[]{:S(2)}) copy-start(f32[1,128]{1,0:T(1,128)} %get-tuple-element.13) | copy-start | bytes 1540
  56.1 0.8 copy-start.4
  60.6 19.3 %collective-permute-start.1 = (bf16[24,9216]{1,0:T(8,128)(2,1)}, bf16[24,9216]{1,0:T(8,128)(2,1)S(1)}, u32[]{:S(2)}, u32[]{:S(2)}) collective-permute-start(bf16[24,9216]{1,0:T(8,128)(2,1)} %get-tuple-element.11), channel_id=1, source_target_pairs={{0,28},{4,0},{8,4},{12,8},{16,12},{20,16},{24,20},{28,24},{1,29},{... | collective-permute-start | bytes 1327112 | tf_op jit(solution)/shard_map/ppermute | solution.py:18
  63.5 9.0 %collective-permute-start.2 = (f32[]{:T(128)}, f32[]{:T(128)}, u32[]{:S(2)}, u32[]{:S(2)}) collective-permute-start(f32[]{:T(128)} %reduce_sum.19), channel_id=1, source_target_pairs={{0,28},{4,0},{8,4},{12,8},{16,12},{20,16},{24,20},{28,24},{1,29},{... | collective-permute-start | bytes 20 | tf_op jit(solution)/shard_map/ppermute | solution.py:18
